TPU v7x, 32 devices: a whole 2x2x4 slice. The times are simulated.
32 devices in a mesh: sector: 4 (over y, core), ops: 8 (over z, x).
Axes of the slice: x: 2, y: 2, z: 4, core: 2. Of those that a mesh axis runs over, the one named last changes fastest.
Arguments:
- wavefunction: bfloat16 [4, 1024, 1024], P('sector', 'ops'), may hold values from -6 to 6
- diag_scale: float32 [4, 1024, 1024], P('sector', 'ops'), may hold values from 1 to 8
- sector_dims: int32 [4], P('sector'), may hold values from 512 to 1024
- left_ops: bfloat16 [4, 16, 1024, 1024], P('sector', 'ops'), may hold values from -0.1875 to 0.1875
- right_ops: bfloat16 [4, 16, 1024, 1024], P('sector', 'ops'), may hold values from -0.1875 to 0.1875
- weight_index: int32 [4, 16], P('sector', 'ops'), may hold values from 0 to 15
- weight_table: float32 [16], replicated, may hold values from -1 to 1
Outputs:
- basis: bfloat16 [4, 1024, 1024], P('sector', 'ops')
- energy: float32 [4], P('sector')
- next_ops: float32 [1024, 1024], P('ops')
All inputs are finite; a program needn't handle non-finite values.
Results may differ from a plain program's by a relative error of at most 0.025.
Values may be sent and summed in bfloat16 or wider, within the bound.
A program may use at most 128 MiB of HBM per device.

v0:
```python
import jax
import jax.numpy as jnp
from jax import lax
from jax.sharding import PartitionSpec as P

KEEP = 1024


def shards(wavefunction, diag_scale, sector_dims, left_ops, right_ops, weight_index, weight_table):
    psi_local = wavefunction[0]
    rows_dev = psi_local.shape[0]
    order_k = psi_local.shape[1]
    pair_count = left_ops.shape[1]
    first_row = lax.axis_index("ops") * rows_dev
    dim = sector_dims[0]
    col_live = jnp.arange(order_k) < dim
    row_live = first_row + jnp.arange(rows_dev) < dim
    psi_masked = jnp.where(
        row_live[:, None] & col_live[None, :], psi_local, jnp.zeros_like(psi_local)
    )
    whole_psi = lax.all_gather(psi_masked, "ops", axis=0, tiled=True)
    onehot = (weight_index[0][:, None] == jnp.arange(weight_table.shape[0])[None, :]).astype(
        jnp.float32
    )
    coef = jnp.sum(onehot * weight_table[None, :], axis=1)
    total = jnp.zeros((lax.axis_size("ops") * rows_dev, order_k), jnp.float32)
    for sigma_pair in range(pair_count):
        left_rows = left_ops[0, sigma_pair]
        applied = jnp.dot(left_rows, whole_psi, preferred_element_type=jnp.float32).astype(
            jnp.bfloat16
        )
        term = lax.dot_general(
            applied,
            right_ops[0, sigma_pair],
            (((1,), (1,)), ((), ())),
            preferred_element_type=jnp.float32,
        )
        total = total + coef[sigma_pair] * term
    live_rows = jnp.arange(lax.axis_size("ops") * rows_dev) < dim
    sigma = lax.psum_scatter(
        jnp.where(live_rows[:, None] & col_live[None, :], total, jnp.float32(0.0)),
        "ops",
        scatter_dimension=0,
        tiled=True,
    )
    psi_f = psi_masked.astype(jnp.float32)
    numer, denom = lax.psum((jnp.sum(psi_f * sigma), jnp.sum(psi_f * psi_f)), "ops")
    energy = numer / denom
    update = psi_f + (sigma - energy * psi_f) / diag_scale[0]
    gram = lax.psum(jnp.dot(update.T, update, precision=lax.Precision.HIGHEST), "ops") / order_k
    gram = gram + 0.001 * jnp.eye(KEEP, dtype=jnp.float32)
    factor = jnp.linalg.cholesky(gram)
    basis_local = jax.scipy.linalg.solve_triangular(factor, update.T, lower=True).T.astype(
        jnp.bfloat16
    )
    basis_full = lax.all_gather(basis_local, "ops", axis=0, tiled=True)
    summed = jnp.zeros((KEEP, KEEP), jnp.float32)
    for pair in range(pair_count):
        moved = jnp.dot(left_ops[0, pair], basis_full, preferred_element_type=jnp.float32).astype(
            jnp.bfloat16
        )
        rotated = jnp.dot(basis_full.T, moved, preferred_element_type=jnp.float32) / order_k
        summed = summed + coef[pair] * rotated
    crossed = lax.psum(summed.astype(jnp.bfloat16), "sector")
    next_rows = lax.psum_scatter(crossed, "ops", scatter_dimension=0, tiled=True).astype(
        jnp.float32
    )
    return (basis_local[None], jnp.reshape(energy, (1,)), next_rows)


def solution(mesh):
    in_specs = (
        P("sector", "ops", None),
        P("sector", "ops", None),
        P("sector"),
        P("sector", "ops", None, None),
        P("sector", "ops", None, None),
        P("sector", "ops"),
        P(),
    )
    out_specs = (P("sector", "ops", None), P("sector"), P("ops", None))
    return jax.shard_map(shards, mesh=mesh, in_specs=in_specs, out_specs=out_specs, check_vma=False)
```

profile of v0, /device:TPU:0, one launch (start us, length us, event | category | flops | bytes accessed | tf_op | source)
XLA Modules:
  0.0 891.9 jit_solution(13805418617051590877)
XLA Ops:
  7.2 1.1 copy.33
  11.5 52.2 %all-gather.3.cloned.1.call-done = bf16[1024,1024]{0,1:T(8,128)(2,1)} async-done(((bf16[128,1024]{0,1:T(8,128)(2,1)}), bf16[1024,1024]{0,1:T(8,128)(2,1)}) %all-gather.3.cloned.1.call-update) | async-done | bytes 2097168 | tf_op jit(solution)/shard_map/all_gather | solution.py:21
  63.7 9.3 %fusion.6 = f32[1024,1024]{0,1:T(8,128)} fusion(bf16[1,2,1024,1024]{3,2,1,0:T(8,128)(2,1)} %param.11, bf16[1024,1024]{0,1:T(8,128)(2,1)} %all-gather.3.cloned.1.call-done, bf16[1,2,1024,1024]{3,2,1,0:T(8,128)(2,1)} %param.10), kind=kOutput, calls=%fused_computation.15 | convolution fusion | flops 4296015872 | bytes 10485760 | tf_op jit(solution)/shard_map/dot_general | solution.py:32
  73.0 12.0 %add_select_fusion = f32[1024,1024]{0,1:T(8,128)} fusion(f32[1024,1024]{0,1:T(8,128)} %fusion.6, bf16[1,2,1024,1024]{3,2,1,0:T(8,128)(2,1)} %param.11, f32[]{:T(128)} %bitcast.6, f32[]{:T(128)} %bitcast.3, pred[1024]{0:T(1024)(128)(4,1)S(1)} %iota_compare_fusion.4, bf16[1024,1024]{0,1:T(8,128)(2,1)} %all-gather.3.cloned.1.call-done, ...), kind=kOutput, calls=%fused_computation.8 | convolution fusion | flops 4301258752 | bytes 14683136 | tf_op jit(solution)/shard_map/dot_general | solution.py:32
  86.3 85.8 %reduce-scatter.3.cloned.1.call-done = f32[128,1024]{0,1:T(8,128)} async-done(((f32[1024,1024]{0,1:T(8,128)}), f32[128,1024]{0,1:T(8,128)}) %reduce-scatter.3.cloned.1.call-update) | async-done | bytes 524304 | tf_op jit(solution)/shard_map/reduce_scatter | solution.py:40
  172.1 1.9 fusion.46
  174.0 32.6 %all-reduce.1 = (f32[]{:T(128)}, f32[]{:T(128)}) all-reduce(f32[]{:T(128)} %get-tuple-element.26, f32[]{:T(128)} %get-tuple-element.25), channel_id=1, replica_groups=mesh['sector'=4,'ops'=8] {'ops'}, use_global_device_ids=true, to_apply=%region_3.4 | all-reduce | flops 2 | bytes 16 | tf_op jit(solution)/shard_map/psum | solution.py:47
  207.9 6.7 fusion.106
  215.0 153.5 %all-reduce.5.cloned.1.call-done = f32[1024,1024]{0,1:T(8,128)} async-done(((f32[1024,1024]{0,1:T(8,128)}), f32[1024,1024]{0,1:T(8,128)}) %all-reduce.5.cloned.1.call-update) | async-done | bytes 4194320 | tf_op jit(solution)/shard_map/psum | solution.py:50
  368.5 5.0 select_add_fusion
  373.5 5.3 copy.38
  378.9 4.5 fusion
  383.4 1.9 copy-done.1
  385.3 11.7 %cholesky.222 = f32[128,128]{1,0:T(8,128)S(1)} custom-call(f32[128,128]{1,0:T(8,128)S(1)} %cholesky.577), custom_call_target="Cholesky" | custom-call | tf_op jit(solution)/shard_map/jit(cholesky)/cholesky | solution.py:52
  397.1 9.8 %custom-call.63 = f32[1,128,128]{1,2,0:T(8,128)S(1)} custom-call(f32[1,128,128]{2,1,0:T(8,128)S(1)} %get-tuple-element.69), custom_call_target="InvertDiagBlocksLowerTriangular" | custom-call | tf_op jit(solution)/shard_map/jit(cholesky)/cholesky | solution.py:52
  407.0 1.5 fusion.51
  408.7 1.6 convolution_subtract_fusion
  410.3 11.7 %cholesky.243 = f32[128,128]{1,0:T(8,128)S(1)} custom-call(f32[128,128]{1,0:T(8,128)S(1)} %cholesky.581), custom_call_target="Cholesky" | custom-call | tf_op jit(solution)/shard_map/jit(cholesky)/cholesky | solution.py:52
  422.5 9.8 %custom-call.64 = f32[1,128,128]{1,2,0:T(8,128)S(1)} custom-call(f32[1,128,128]{2,1,0:T(8,128)S(1)} %get-tuple-element.67), custom_call_target="InvertDiagBlocksLowerTriangular" | custom-call | tf_op jit(solution)/shard_map/jit(cholesky)/cholesky | solution.py:52
  433.4 2.0 copy-done
  435.4 2.4 convolution_subtract_fusion.1
  437.8 11.7 %cholesky.466 = f32[128,128]{1,0:T(8,128)S(1)} custom-call(f32[128,128]{1,0:T(8,128)S(1)} %cholesky.586), custom_call_target="Cholesky" | custom-call | tf_op jit(solution)/shard_map/jit(cholesky)/cholesky | solution.py:52
  450.3 9.8 %custom-call.65 = f32[1,128,128]{1,2,0:T(8,128)S(1)} custom-call(f32[1,128,128]{2,1,0:T(8,128)S(1)} %get-tuple-element.65), custom_call_target="InvertDiagBlocksLowerTriangular" | custom-call | tf_op jit(solution)/shard_map/jit(cholesky)/cholesky | solution.py:52
  460.1 1.3 convolution_dynamic-update-slice_fusion.1
  461.4 3.3 convolution_subtract_fusion.2
  464.7 11.7 %cholesky.485 = f32[128,128]{1,0:T(8,128)S(1)} custom-call(f32[128,128]{1,0:T(8,128)S(1)} %cholesky.591), custom_call_target="Cholesky" | custom-call | tf_op jit(solution)/shard_map/jit(cholesky)/cholesky | solution.py:52
  477.2 9.8 %custom-call.66 = f32[1,128,128]{1,2,0:T(8,128)S(1)} custom-call(f32[1,128,128]{2,1,0:T(8,128)S(1)} %get-tuple-element.63), custom_call_target="InvertDiagBlocksLowerTriangular" | custom-call | tf_op jit(solution)/shard_map/jit(cholesky)/cholesky | solution.py:52
  487.0 1.1 convolution_dynamic-update-slice_fusion.2
  488.1 3.1 convolution_subtract_fusion.3
  491.3 11.9 %cholesky.504 = f32[128,128]{1,0:T(8,128)S(1)} custom-call(f32[128,128]{1,0:T(8,128)S(1)} %cholesky.596), custom_call_target="Cholesky" | custom-call | tf_op jit(solution)/shard_map/jit(cholesky)/cholesky | solution.py:52
  504.0 9.8 %custom-call.67 = f32[1,128,128]{1,2,0:T(8,128)S(1)} custom-call(f32[1,128,128]{2,1,0:T(8,128)S(1)} %get-tuple-element.61), custom_call_target="InvertDiagBlocksLowerTriangular" | custom-call | tf_op jit(solution)/shard_map/jit(cholesky)/cholesky | solution.py:52
  513.8 1.1 convolution_dynamic-update-slice_fusion.3
  514.9 3.1 convolution_subtract_fusion.4
  518.0 11.7 %cholesky.524 = f32[128,128]{1,0:T(8,128)S(1)} custom-call(f32[128,128]{1,0:T(8,128)S(1)} %cholesky.601), custom_call_target="Cholesky" | custom-call | tf_op jit(solution)/shard_map/jit(cholesky)/cholesky | solution.py:52
  530.5 9.8 %custom-call.68 = f32[1,128,128]{1,2,0:T(8,128)S(1)} custom-call(f32[1,128,128]{2,1,0:T(8,128)S(1)} %get-tuple-element.59), custom_call_target="InvertDiagBlocksLowerTriangular" | custom-call | tf_op jit(solution)/shard_map/jit(cholesky)/cholesky | solution.py:52
  541.3 3.1 convolution_subtract_fusion.5
  544.4 11.7 %cholesky.544 = f32[128,128]{1,0:T(8,128)S(1)} custom-call(f32[128,128]{1,0:T(8,128)S(1)} %cholesky.606), custom_call_target="Cholesky" | custom-call | tf_op jit(solution)/shard_map/jit(cholesky)/cholesky | solution.py:52
  556.9 9.8 %custom-call.69 = f32[1,128,128]{1,2,0:T(8,128)S(1)} custom-call(f32[1,128,128]{2,1,0:T(8,128)S(1)} %get-tuple-element.57), custom_call_target="InvertDiagBlocksLowerTriangular" | custom-call | tf_op jit(solution)/shard_map/jit(cholesky)/cholesky | solution.py:52
  567.6 2.1 convolution_subtract_fusion.11
  569.7 11.7 %cholesky.562 = f32[128,128]{1,0:T(8,128)S(1)} custom-call(f32[128,128]{1,0:T(8,128)S(1)} %convolution_subtract_fusion.11), custom_call_target="Cholesky" | custom-call | tf_op jit(solution)/shard_map/jit(cholesky)/cholesky | solution.py:52
  591.9 4.8 select_select_fusion
  596.7 23.7 %while.1 = (s32[]{:T(128)}, f32[1024,1024]{0,1:T(8,128)}, s32[8,2]{0,1:T(2,128)S(1)}, f32[8,128,128]{2,1,0:T(8,128)S(1)}, s32[]{:T(128)}) while((s32[]{:T(128)}, f32[1024,1024]{0,1:T(8,128)}, s32[8,2]{0,1:T(2,128)S(1)}, f32[8,128,128]{2,1,0:T(8,128)S(1)}, s32[]{:T(128)}) %tuple.55), condition=%wide.while_cond, body=%wide.while_body.sunk | while | flops 2 | bytes 393329 | solution.py:53
  597.4 2.2 dynamic-slice.7
  600.3 2.2 dynamic-slice.7
  603.3 2.2 dynamic-slice.7
  606.3 2.2 dynamic-slice.7
  609.3 2.2 dynamic-slice.7
  612.3 2.2 dynamic-slice.7
  615.2 2.2 dynamic-slice.7
  618.2 2.2 dynamic-slice.7
  620.5 78.8 %custom-call.70 = f32[8,128,128]{1,2,0:T(8,128)S(1)} custom-call(f32[8,128,128]{2,1,0:T(8,128)S(1)} %get-tuple-element.10), custom_call_target="InvertDiagBlocksLowerTriangular" | custom-call | tf_op jit(solution)/shard_map/jit(_solve_triangular)/triangular_solve | solution.py:53
  699.6 1.1 convolution_subtract_fusion.10
  701.0 1.3 convolution_subtract_fusion.9
  702.6 1.4 convolution_subtract_fusion.13
  704.4 1.5 convolution_subtract_fusion.12
  706.3 1.7 convolution_subtract_fusion.8
  708.3 1.8 convolution_subtract_fusion.7
  710.4 1.9 convolution_subtract_fusion.6
  714.9 48.0 %all-gather.5.cloned.1.call-done = bf16[1024,1024]{0,1:T(8,128)(2,1)} async-done(((bf16[128,1024]{0,1:T(8,128)(2,1)}), bf16[1024,1024]{0,1:T(8,128)(2,1)}) %all-gather.5.cloned.1.call-update) | async-done | bytes 2097168 | tf_op jit(solution)/shard_map/all_gather | solution.py:56
  762.9 9.5 %fusion.13 = f32[1024,1024]{1,0:T(8,128)} fusion(bf16[1024,1024]{0,1:T(8,128)(2,1)} %all-gather.5.cloned.1.call-done, bf16[1,2,1024,1024]{3,2,1,0:T(8,128)(2,1)} %param.10), kind=kOutput, calls=%fused_computation.22 | convolution fusion | flops 4296015872 | bytes 10485760 | tf_op jit(solution)/shard_map/dot_general | solution.py:62
  772.3 8.7 add_convert_fusion
  781.1 67.3 %reduce-scatter.5.cloned.1.call-done = bf16[128,1024]{1,0:T(8,128)(2,1)} async-done(((bf16[1024,1024]{1,0:T(8,128)(2,1)}), bf16[128,1024]{1,0:T(8,128)(2,1)}) %reduce-scatter.5.cloned.1.call-update) | async-done | bytes 262160 | tf_op jit(solution)/shard_map/reduce_scatter | solution.py:65
  849.3 32.7 %all-reduce.7.cloned.1.call-done = bf16[128,1024]{1,0:T(8,128)(2,1)} async-done(((bf16[128,1024]{1,0:T(8,128)(2,1)}), bf16[128,1024]{1,0:T(8,128)(2,1)}) %all-reduce.7.cloned.1.call-update) | async-done | bytes 262160 | tf_op jit(solution)/shard_map/psum | solution.py:64
  881.9 1.8 convert_element_type.38
  (127 shorter events, 27.4 us)
Async XLA Ops:
  7.2 56.5 %all-gather.3.cloned.1.call-start = ((), (), s32[]{:S(2)}) async-start(), calls=%async_computation.2 | async-start | bytes 2359296 | tf_op jit(solution)/shard_map/all_gather | solution.py:21
  10.0 162.1 %reduce-scatter.3.cloned.1.call-start = ((), (), s32[]{:S(2)}) async-start(), calls=%async_computation.3 | async-start | bytes 4718592 | tf_op jit(solution)/shard_map/reduce_scatter | solution.py:40
  85.0 1.0 copy-start.6
  85.0 122.9 %copy-start.3 = (bf16[128,1024]{0,1:T(8,128)(2,1)S(1)}, bf16[128,1024]{0,1:T(8,128)(2,1)}, u32[]{:S(2)}) copy-start(bf16[128,1024]{0,1:T(8,128)(2,1)} %and_select_fusion) | copy-start | bytes 786436
  85.0 283.5 %all-reduce.5.cloned.1.call-start = ((), (), s32[]{:S(2)}) async-start(), calls=%async_computation.4 | async-start | bytes 8388608 | tf_op jit(solution)/shard_map/psum | solution.py:50
  207.9 6.9 copy-start.2
  214.7 548.2 %all-gather.5.cloned.1.call-start = ((), (), s32[]{:S(2)}) async-start(), calls=%async_computation.5 | async-start | bytes 2359296 | tf_op jit(solution)/shard_map/all_gather | solution.py:56
  383.3 1.9 copy-start.1
  433.4 2.0 copy-start
  712.6 0.7 copy-start.4
  713.4 135.0 %reduce-scatter.5.cloned.1.call-start = ((), (), s32[]{:S(2)}) async-start(), calls=%async_computation.6 | async-start | bytes 2359296 | tf_op jit(solution)/shard_map/reduce_scatter | solution.py:65
  762.9 9.5 %copy-start.7 = (bf16[1024,1024]{0,1:T(8,128)(2,1)S(1)}, bf16[1024,1024]{0,1:T(8,128)(2,1)}, u32[]{:S(2)}) copy-start(bf16[1024,1024]{0,1:T(8,128)(2,1)} %all-gather.5.cloned.1.call-done) | copy-start | bytes 6291460
  772.3 76.1 %copy-start.5 = (bf16[1024,128]{1,0:T(8,128)(2,1)S(1)}, bf16[1024,128]{1,0:T(8,128)(2,1)}, u32[]{:S(2)}) copy-start(bf16[1024,128]{1,0:T(8,128)(2,1)} %copy-done.4) | copy-start | bytes 786436
  781.1 100.8 %all-reduce.7.cloned.1.call-start = ((), (), s32[]{:S(2)}) async-start(), calls=%async_computation.7 | async-start | bytes 524288 | tf_op jit(solution)/shard_map/psum | solution.py:64
Sparse Core Ops, SparseCore 0:
  10.6 53.0 all-gather.2
  85.2 86.8 reduce-scatter.2
  214.8 153.6 all-reduce.4
  713.5 49.3 all-gather.4
  781.2 67.1 reduce-scatter.4
  850.6 31.3 all-reduce.6
where the time goes:
time: 899 us; the launch traced here: 892 us
  waiting for transfers between devices  440 us (49%)
  other arithmetic  266 us (30%)
  matrix products  85.5 us (10%)
  local copies, waits for them, and re-layouts  43.1 us (5%)
  blocking collectives  32.6 us (4%)
  between operations  24.2 us (3%)
    another operation x30, other arithmetic, shards(): factor = jnp.linalg.cholesky(gram)  168 us
    psum x1, waiting for transfers between devices, shards(): lax.psum(jnp.dot(update.T, update, precision=lax.Precision.HIGHEST), 'ops')  154 us
    reduce_scatter x1, waiting for transfers between devices, shards(): lax.psum_scatter(jnp.where(live_rows[:, None] & col_live[None, :], total,...  85.8 us
    another operation x3, other arithmetic, shards(): jax.scipy.linalg.solve_triangular(factor, update.T, lower=True)  83.6 us
    reduce_scatter x1, waiting for transfers between devices, shards(): lax.psum_scatter(crossed, 'ops', scatter_dimension=0, tiled=True)  67.3 us
    all_gather x1, waiting for transfers between devices, shards(): whole_psi = lax.all_gather(psi_masked, 'ops', axis=0, tiled=True)  52.2 us
    all_gather x1, waiting for transfers between devices, shards(): basis_full = lax.all_gather(basis_local, 'ops', axis=0, tiled=True)  48 us
    psum x1, waiting for transfers between devices, shards(): crossed = lax.psum(summed.astype(jnp.bfloat16), 'sector')  32.7 us
  transfers between devices with their start and end apart: 6, of which 6 were waited for; matrix products, arithmetic and copies ran while one was open for 0% of the time, Pallas kernels for 0%

commit v1 on v0

v1 whole, which is shorter than its diff:
```python
import functools

import jax
import jax.numpy as jnp
from jax import lax
from jax.experimental import pallas as pl
from jax.experimental.pallas import tpu as pltpu
from jax.sharding import PartitionSpec as P

BLOCK = 128
SUB = 8


def split3(u):
    high = u.astype(jnp.bfloat16).astype(jnp.float32)
    rest = u - high
    mid = rest.astype(jnp.bfloat16).astype(jnp.float32)
    low = (rest - mid).astype(jnp.bfloat16).astype(jnp.float32)
    return high, mid, low


def inverse_factor(block):
    size = block.shape[0]
    lane = lax.broadcasted_iota(jnp.int32, (SUB, size), 1)
    row = lax.broadcasted_iota(jnp.int32, (SUB, size), 0)
    below = block
    done = []
    for s in range(size // SUB):
        at = s * SUB
        top = below[:SUB]
        columns = [
            jnp.broadcast_to(top[:, at + j : at + j + 1], (SUB, size)) for j in range(SUB)
        ]
        here = (lane >= at) & (lane < at + SUB)
        body = jnp.where(here, (lane - at == row).astype(jnp.float32), top)
        pivots = jnp.ones((SUB, size), jnp.float32)
        for j in range(SUB):
            pivot = jnp.broadcast_to(columns[j][j : j + 1], (SUB, size))
            pivots = jnp.where(row == j, pivot, pivots)
            if j < SUB - 1:
                factor = jnp.where(row > j, columns[j] / pivot, 0.0)
                for c in range(j + 1, SUB):
                    columns[c] = columns[c] - factor * columns[c][j : j + 1]
                body = body - factor * body[j : j + 1]
        scaled = body * lax.rsqrt(pivots)
        done.append(scaled)
        if at + SUB < size:
            high, mid, low = split3(scaled)
            left = jnp.concatenate([high, high, mid, high, mid, low], axis=0)
            right = jnp.concatenate([high, mid, high, low, mid, high], axis=0)
            outer = lax.dot_general(
                left.T.astype(jnp.bfloat16),
                right.astype(jnp.bfloat16),
                (((1,), (0,)), ((), ())),
                preferred_element_type=jnp.float32,
            )
            rows_left = size - at - SUB
            lanes = lax.broadcasted_iota(jnp.int32, (rows_left, size), 1)
            kept = jnp.where((lanes >= at) & (lanes < at + SUB), 0.0, below[SUB:])
            below = kept - outer[at + SUB :]
    whole = jnp.concatenate(done, axis=0)
    r = lax.broadcasted_iota(jnp.int32, (size, size), 0)
    c = lax.broadcasted_iota(jnp.int32, (size, size), 1)
    return jnp.where(c <= r, whole, 0.0)


def inverse_kernel(scale, gram_ref, high_ref, low_ref, work):
    order = gram_ref.shape[0]
    blocks = order // BLOCK
    column = lax.broadcasted_iota(jnp.int32, (BLOCK, order), 1)
    local = lax.broadcasted_iota(jnp.int32, (BLOCK, order), 0)

    def rows(i):
        return pl.ds(pl.multiple_of(i * BLOCK, BLOCK), BLOCK)

    def load(i, carry):
        eye = (column == local + i * BLOCK).astype(jnp.float32)
        work[rows(i), :] = gram_ref[rows(i), :] * scale + 0.001 * eye
        return carry

    lax.fori_loop(0, blocks, load, 0)

    def step(k, carry):
        first = k * BLOCK
        inverse = inverse_factor(work[rows(k), rows(k)])
        in_k = (column >= first) & (column < first + BLOCK)
        pivot_rows = jnp.where(
            in_k, (column - first == local).astype(jnp.float32), work[rows(k), :]
        )
        work[rows(k), :] = jnp.dot(
            inverse,
            pivot_rows,
            precision=lax.Precision.HIGHEST,
            preferred_element_type=jnp.float32,
        )

        def update(i, inner):
            panel = work[rows(k), rows(i)].T
            kept = jnp.where(in_k, 0.0, work[rows(i), :])
            work[rows(i), :] = kept - jnp.dot(
                panel,
                work[rows(k), :],
                precision=lax.Precision.HIGHEST,
                preferred_element_type=jnp.float32,
            )
            return inner

        lax.fori_loop(k + 1, blocks, update, 0)
        return carry

    lax.fori_loop(0, blocks, step, 0)

    def store(i, carry):
        kept = jnp.where(column <= local + i * BLOCK, work[rows(i), :], 0.0)
        high = kept.astype(jnp.bfloat16)
        high_ref[rows(i), :] = high
        low_ref[rows(i), :] = (kept - high.astype(jnp.float32)).astype(jnp.bfloat16)
        return carry

    lax.fori_loop(0, blocks, store, 0)


def inverse_cholesky(product, scale):
    order = product.shape[0]
    half = jax.ShapeDtypeStruct((order, order), jnp.bfloat16)
    vmem = pl.BlockSpec(memory_space=pltpu.VMEM)
    return pl.pallas_call(
        functools.partial(inverse_kernel, scale),
        out_shape=(half, half),
        in_specs=[vmem],
        out_specs=(vmem, vmem),
        scratch_shapes=[pltpu.VMEM((order, order), jnp.float32)],
        compiler_params=pltpu.CompilerParams(vmem_limit_bytes=40 * 2**20),
        cost_estimate=pl.CostEstimate(
            flops=400 * order**3 // 10, bytes_accessed=8 * order**2, transcendentals=0
        ),
        name="inverse_cholesky",
    )(product)


def shards(wavefunction, diag_scale, sector_dims, left_ops, right_ops, weight_index, weight_table):
    psi_local = wavefunction[0]
    rows_dev = psi_local.shape[0]
    order_k = psi_local.shape[1]
    pair_count = left_ops.shape[1]
    owners = lax.axis_size("ops")
    first_row = lax.axis_index("ops") * rows_dev
    dim = sector_dims[0]
    live = jnp.arange(order_k) < dim
    both = live[:, None] & live[None, :]
    whole_psi = lax.all_gather(psi_local, "ops", axis=0, tiled=True)
    whole_psi = jnp.where(both, whole_psi, jnp.zeros_like(whole_psi))
    onehot = (weight_index[0][:, None] == jnp.arange(weight_table.shape[0])[None, :]).astype(
        jnp.float32
    )
    coef = jnp.sum(onehot * weight_table[None, :], axis=1)

    total = jnp.zeros((order_k, order_k), jnp.float32)
    operator = jnp.zeros((order_k, order_k), jnp.float32)
    for pair in range(pair_count):
        applied = jnp.dot(
            left_ops[0, pair], whole_psi, preferred_element_type=jnp.float32
        ).astype(jnp.bfloat16)
        term = lax.dot_general(
            applied,
            right_ops[0, pair],
            (((1,), (1,)), ((), ())),
            preferred_element_type=jnp.float32,
        )
        total = total + coef[pair] * term
        operator = operator + coef[pair] * left_ops[0, pair].astype(jnp.float32)
    total = jnp.where(both, total, jnp.float32(0.0))
    whole_f = whole_psi.astype(jnp.float32)
    partial_numer = jnp.sum(whole_f * total)
    denom = jnp.sum(whole_f * whole_f)
    packed = jnp.concatenate(
        [
            total.reshape(owners, rows_dev, order_k),
            jnp.full((owners, SUB, order_k), partial_numer),
        ],
        axis=1,
    ).reshape(owners * (rows_dev + SUB), order_k)
    summed = lax.psum_scatter(packed, "ops", scatter_dimension=0, tiled=True)
    sigma = summed[:rows_dev]
    energy = summed[rows_dev, 0] / denom

    row_live = first_row + jnp.arange(rows_dev) < dim
    psi_f = jnp.where(row_live[:, None] & live[None, :], psi_local, 0).astype(jnp.float32)
    update = psi_f + (sigma - energy * psi_f) / diag_scale[0]
    columns = lax.all_gather(update.astype(jnp.bfloat16), "ops", axis=0, tiled=True)

    operator, columns = lax.optimization_barrier((operator.astype(jnp.bfloat16), columns))
    operator = lax.psum(operator, "ops")

    product = lax.dot_general(
        columns, columns, (((0,), (0,)), ((), ())), preferred_element_type=jnp.float32
    )
    high, low = inverse_cholesky(product, 1.0 / order_k)
    across = (((1,), (1,)), ((), ()))
    basis = (
        lax.dot_general(columns, high, across, preferred_element_type=jnp.float32)
        + lax.dot_general(columns, low, across, preferred_element_type=jnp.float32)
    ).astype(jnp.bfloat16)
    basis_local = lax.dynamic_slice_in_dim(basis, first_row, rows_dev, axis=0)

    own = lax.dynamic_slice_in_dim(basis, first_row, rows_dev, axis=1)
    half = lax.dot_general(
        own, operator, (((0,), (0,)), ((), ())), preferred_element_type=jnp.float32
    ).astype(jnp.bfloat16)
    rotated = jnp.dot(half, basis, preferred_element_type=jnp.float32) / order_k
    next_rows = lax.psum(rotated.astype(jnp.bfloat16), "sector").astype(jnp.float32)
    return (basis_local[None], jnp.reshape(energy, (1,)), next_rows)


def solution(mesh):
    in_specs = (
        P("sector", "ops", None),
        P("sector", "ops", None),
        P("sector"),
        P("sector", "ops", None, None),
        P("sector", "ops", None, None),
        P("sector", "ops"),
        P(),
    )
    out_specs = (P("sector", "ops", None), P("sector"), P("ops", None))
    return jax.shard_map(shards, mesh=mesh, in_specs=in_specs, out_specs=out_specs, check_vma=False)
```

time: 899 us -> 385 us (0.43)
  other arithmetic: 266 us -> 10.5 us
  waiting for transfers between devices: 440 us -> 242 us
  Pallas kernels: 0 us -> 71.6 us
  matrix products: 85.5 us -> 33.6 us
  local copies, waits for them, and re-layouts: 43.1 us -> 9.46 us
  blocking collectives: 32.6 us -> 0 us
    another operation x33 -> x0, other arithmetic: 251 us -> none  [the longest x30 168 us: shards(): factor = jnp.linalg.cholesky(gram)]
    psum x2, waiting for transfers between devices: 186 us -> 55.7 us  [the longest x1 31 us: shards(): lax.psum(rotated.astype(jnp.bfloat16), 'sector').astype(jnp.float32)]
    pallas_call x0 -> x1, Pallas kernels: none -> 71.6 us  [inverse_cholesky(): pl.pallas_call(functools.partial(inverse_kernel, scale), out_shape=(half,...]
    reduce_scatter x2 -> x1, waiting for transfers between devices: 153 us -> 90.6 us  [shards(): summed = lax.psum_scatter(packed, 'ops', scatter_dimension=0, tiled=True)]
    another operation x29 -> x0, matrix products: 39.3 us -> none  [the longest x14 26.1 us: shards(): factor = jnp.linalg.cholesky(gram)]
    psum x1 -> x0, blocking collectives: 32.6 us -> none  [shards(): lax.psum((jnp.sum(psi_f * sigma), jnp.sum(psi_f * psi_f)), 'ops')]
    another operation x67 -> x0, local copies, waits for them, and re-layouts: 29.3 us -> none
    dot_general x5 -> x6, matrix products: 46.3 us -> 33.6 us  [the longest x2 23.3 us: shards(): lax.dot_general(applied, right_ops[0, pair], (((1,), (1,)), ((), ())), pr...]
  transfers between devices with their start and end apart: 6 -> 5, of which waited for: 6 -> 5; matrix products, arithmetic and copies ran while one was open for 0% -> 4% of each run, Pallas kernels for 0% -> 19%
where the time goes in v1:
time: 385 us; the launch traced here: 384 us
  waiting for transfers between devices  242 us (63%)
  Pallas kernels  71.6 us (19%)
  matrix products  33.6 us (9%)
  between operations  17 us (4%)
  other arithmetic  10.5 us (3%)
  local copies, waits for them, and re-layouts  9.46 us (2%)
    reduce_scatter x1, waiting for transfers between devices, shards(): summed = lax.psum_scatter(packed, 'ops', scatter_dimension=0, tiled=True)  90.6 us
    pallas_call x1, Pallas kernels, inverse_cholesky(): pl.pallas_call(functools.partial(inverse_kernel, scale), out_shape=(half,...  71.6 us
    all_gather x1, waiting for transfers between devices, shards(): whole_psi = lax.all_gather(psi_local, 'ops', axis=0, tiled=True)  51.8 us
    all_gather x1, waiting for transfers between devices, shards(): lax.all_gather(update.astype(jnp.bfloat16), 'ops', axis=0, tiled=True)  42.8 us
    psum x1, waiting for transfers between devices, shards(): lax.psum(rotated.astype(jnp.bfloat16), 'sector').astype(jnp.float32)  31 us
    psum x1, waiting for transfers between devices, shards(): operator = lax.psum(operator, 'ops')  24.7 us
    dot_general x2, matrix products, shards(): lax.dot_general(applied, right_ops[0, pair], (((1,), (1,)), ((), ())), pr...  23.3 us
  transfers between devices with their start and end apart: 5, of which 5 were waited for; matrix products, arithmetic and copies ran while one was open for 4% of the time, Pallas kernels for 19%

profile of v1, /device:TPU:0, one launch (start us, length us, event | category | flops | bytes accessed | tf_op | source)
XLA Modules:
  0.0 384.1 jit_solution(1623291549600917774)
XLA Ops:
  7.2 0.0 all-gather.6.cloned.1.call-start
  7.2 0.7 all-gather.6.cloned.1.call-update
  7.9 0.0 reduce-scatter.2.cloned.1.call-start
  8.6 0.9 fusion.29
  9.5 0.7 fusion.32
  10.1 51.8 %all-gather.6.cloned.1.call-done = bf16[1,1024,1024]{2,1,0:T(8,128)(2,1)} async-done(((bf16[1,128,1024]{2,1,0:T(8,128)(2,1)}), bf16[1,1024,1024]{2,1,0:T(8,128)(2,1)}) %all-gather.6.cloned.1.call-update) | async-done | bytes 2097168 | tf_op jit(solution)/shard_map/all_gather | solution.py:151
  61.9 0.0 copy-start.4
  61.9 9.8 %fusion.3 = f32[1024,1024]{1,0:T(8,128)} fusion(bf16[1,2,1024,1024]{3,2,1,0:T(8,128)(2,1)} %param.11, bf16[1,2,1024,1024]{3,2,1,0:T(8,128)(2,1)} %param.10, bf16[1,1024,1024]{2,1,0:T(8,128)(2,1)} %all-gather.6.cloned.1.call-done, pred[1024]{0:T(1024)(128)(4,1)S(1)} %iota_compare_fusion), kind=kOutput, calls=%fused_computation.9 | convolution fusion | flops 4298113024 | bytes 10487808 | tf_op jit(solution)/shard_map/dot_general | solution.py:164
  71.7 0.0 copy-done.4
  71.7 13.5 %fusion.1 = (f32[]{:T(128)}, f32[]{:T(128)}, f32[1024,1024]{1,0:T(8,128)}) fusion(bf16[1,1024,1024]{2,1,0:T(8,128)(2,1)S(1)} %copy-done.4, pred[1024]{0:T(1024)(128)(4,1)S(1)} %iota_compare_fusion, bf16[1,2,1024,1024]{3,2,1,0:T(8,128)(2,1)} %param.11, bf16[1,2,1024,1024]{3,2,1,0:T(8,128)(2,1)} %param.10, f32[]{:T(128)} %bitcast.3, f32[1024,1024]{1,0:T(8,128)} %fusion.3, ...), kind=kOutput, calls=%fused_computation.5 | convolution fusion | flops 4309647360 | bytes 16782344 | tf_op jit(solution)/shard_map/dot_general | solution.py:164
  85.3 5.4 %concatenate.3 = f32[8,136,1024]{2,1,0:T(8,128)} pad(f32[8,128,1024]{2,1,0:T(8,128)} %bitcast.65, f32[]{:T(128)} %get-tuple-element.12), padding=0_0x0_8x0_0 | pad | bytes 8650756 | tf_op jit(solution)/shard_map/concatenate | solution.py:176
  90.6 0.0 copy-start
  90.6 0.0 copy-start.1
  90.6 0.0 reduce-scatter.2.cloned.1.call-update
  90.7 0.0 all-gather.4.cloned.1.call-start
  90.7 90.6 %reduce-scatter.2.cloned.1.call-done = f32[136,1024]{1,0:T(8,128)} async-done(((f32[1088,1024]{1,0:T(8,128)}), f32[136,1024]{1,0:T(8,128)}) %reduce-scatter.2.cloned.1.call-update) | async-done | bytes 557072 | tf_op jit(solution)/shard_map/reduce_scatter | solution.py:183
  181.4 1.2 slice.37
  183.9 0.0 copy-done
  183.9 0.0 copy-done.1
  183.9 2.0 fusion.26
  185.9 0.0 all-gather.4.cloned.1.call-update
  185.9 0.2 all-reduce.4.cloned.1.call-start
  186.1 5.9 %add_convert_fusion.1 = bf16[1024,1024]{1,0:T(8,128)(2,1)} fusion(f32[]{:T(128)} %bitcast.3, f32[]{:T(128)} %bitcast.1, bf16[1,2,1024,1024]{3,2,1,0:T(8,128)(2,1)} %param.10), kind=kLoop, calls=%fused_computation.7 | loop fusion | flops 6291456 | bytes 6291464 | tf_op jit(solution)/shard_map/convert_element_type | solution.py:192
  192.0 42.8 %all-gather.4.cloned.1.call-done = bf16[1024,1024]{1,0:T(8,128)(2,1)} async-done(((bf16[128,1024]{1,0:T(8,128)(2,1)}), bf16[1024,1024]{1,0:T(8,128)(2,1)}) %all-gather.4.cloned.1.call-update) | async-done | bytes 2097168 | tf_op jit(solution)/shard_map/all_gather | solution.py:190
  234.8 0.0 copy-start.2
  234.8 0.0 all-reduce.4.cloned.1.call-update
  234.8 0.0 all-reduce.6.cloned.1.call-start
  234.9 1.5 copy-done.2
  236.4 2.4 fusion.35.gram_ref
  238.8 71.6 %inverse_cholesky.1 = (bf16[1024,1024]{1,0:T(8,128)(2,1)S(1)}, bf16[1024,1024]{1,0:T(8,128)(2,1)S(1)}) custom-call(f32[1024,1024]{1,0:T(8,128)S(1)} %fusion.35.gram_ref), custom_call_target="tpu_custom_call" | custom-call | flops 42949672960 | bytes 8388608 | tf_op jit(solution)/shard_map/inverse_cholesky/pallas_call | solution.py:127
  310.3 0.0 copy-start.3
  310.3 2.4 fusion.36
  312.7 0.0 copy-done.3
  312.7 2.4 add_convert_fusion
  315.1 24.7 %all-reduce.4.cloned.1.call-done = bf16[1024,1024]{1,0:T(8,128)(2,1)} async-done(((bf16[1024,1024]{1,0:T(8,128)(2,1)}), bf16[1024,1024]{1,0:T(8,128)(2,1)}) %all-reduce.4.cloned.1.call-update) | async-done | bytes 2097168 | tf_op jit(solution)/shard_map/psum | solution.py:193
  339.8 3.1 fusion.15
  342.9 0.0 all-reduce.6.cloned.1.call-update
  342.9 0.7 dynamic-slice_bitcast_fusion
  343.7 31.0 %all-reduce.6.cloned.1.call-done = bf16[128,1024]{1,0:T(8,128)(2,1)} async-done(((bf16[128,1024]{1,0:T(8,128)(2,1)}), bf16[128,1024]{1,0:T(8,128)(2,1)}) %all-reduce.6.cloned.1.call-update) | async-done | bytes 262160 | tf_op jit(solution)/shard_map/psum | solution.py:211
  374.7 1.8 convert_element_type.52
  (2 shorter events, 0.0 us)
Async XLA Ops:
  7.2 54.8 %all-gather.6.cloned.1.call-start = ((), (), s32[]{:S(2)}) async-start(), calls=%async_computation.5 | async-start | bytes 2359296 | tf_op jit(solution)/shard_map/all_gather | solution.py:151
  7.9 173.5 %reduce-scatter.2.cloned.1.call-start = ((), (), s32[]{:S(2)}) async-start(), calls=%async_computation.1 | async-start | bytes 5013504 | tf_op jit(solution)/shard_map/reduce_scatter | solution.py:183
  61.9 9.8 %copy-start.4 = (bf16[1,1024,1024]{2,1,0:T(8,128)(2,1)S(1)}, bf16[1,1024,1024]{2,1,0:T(8,128)(2,1)}, u32[]{:S(2)}) copy-start(bf16[1,1024,1024]{2,1,0:T(8,128)(2,1)} %all-gather.6.cloned.1.call-done) | copy-start | bytes 6291460
  90.6 93.2 %copy-start = (bf16[1,128,1024]{2,1,0:T(8,128)(2,1)S(1)}, bf16[1,128,1024]{2,1,0:T(8,128)(2,1)}, u32[]{:S(2)}) copy-start(bf16[1,128,1024]{2,1,0:T(8,128)(2,1)} %param.7) | copy-start | bytes 786436
  90.6 93.2 %copy-start.1 = (f32[1,128,1024]{2,1,0:T(8,128)S(1)}, f32[1,128,1024]{2,1,0:T(8,128)}, u32[]{:S(2)}) copy-start(f32[1,128,1024]{2,1,0:T(8,128)} %param.8) | copy-start | bytes 1572868
  90.7 144.1 %all-gather.4.cloned.1.call-start = ((), (), s32[]{:S(2)}) async-start(), calls=%async_computation.2 | async-start | bytes 2359296 | tf_op jit(solution)/shard_map/all_gather | solution.py:190
  185.9 153.9 %all-reduce.4.cloned.1.call-start = ((), (), s32[]{:S(2)}) async-start(), calls=%async_computation.3 | async-start | bytes 4194304 | tf_op jit(solution)/shard_map/psum | solution.py:193
  234.8 1.6 copy-start.2
  234.8 139.8 %all-reduce.6.cloned.1.call-start = ((), (), s32[]{:S(2)}) async-start(), calls=%async_computation.4 | async-start | bytes 524288 | tf_op jit(solution)/shard_map/psum | solution.py:211
  310.3 2.4 copy-start.3
Sparse Core Ops, SparseCore 0:
  10.1 51.7 all-gather.5
  90.8 90.5 reduce-scatter.1
  186.0 48.7 all-gather.3
  238.3 101.4 all-reduce.3
  343.1 31.5 all-reduce.5
